TPU v7x, 32 devices: a whole 2x2x4 slice. The times are simulated.
32 devices in a mesh: dp: 16 (over z, y, core), space: 2 (over x).
Axes of the slice: x: 2, y: 2, z: 4, core: 2. Of those that a mesh axis runs over, the one named last changes fastest.
Arguments:
- feature_map: bfloat16 [16, 24, 84, 256], P('dp', 'space'), may hold values from -6 to 6
- proposals: int32 [16, 128, 4], P('dp'), may hold values from 0 to 84, as said below
- hidden_weight: bfloat16 [12544, 512], P(None, 'space'), may hold values from -0.0546875 to 0.0546875
- output_weight: bfloat16 [512, 512], P('space'), may hold values from -0.25 to 0.25
- upstream: bfloat16 [16, 128, 512], P('dp'), may hold values from -6 to 6
Outputs:
- hidden_weight_grad: float32 [12544, 512], P('dp', 'space')
- output_weight_grad: float32 [512, 512], P('space')
- feature_grad: float32 [16, 24, 84, 256], P('dp', 'space')
Inputs may be any that keep to these rules, and one draw needn't show every extreme that they name: `proposals`: each row holds top, left, bottom, right with top < bottom <= 24 and left < right <= 84.
All inputs are finite; a program needn't handle non-finite values.
Results may differ from a plain program's by a relative error of at most 0.012.
Values may be sent and summed in bfloat16 or wider, within the bound.
No kernel may reach another device: no remote copies, remote signals or barrier semaphores. Data moves between devices by JAX's collectives and lax.ppermute only.
A program may use at most 128 MiB of HBM per device.

v0:
```python
import jax
import jax.numpy as jnp
from jax import lax
from jax.sharding import PartitionSpec as P

POOL = 7


def axis_weights(low_edge, high_edge, grid_points):
    edge_start = low_edge.astype(jnp.float32)
    bin_size = (high_edge - low_edge).astype(jnp.float32) / POOL
    bin_index = jnp.arange(POOL).astype(jnp.float32)
    offsets = jnp.array([0.25, 0.75], jnp.float32)
    sample_points = (
        edge_start[:, None, None]
        + (bin_index[None, :, None] + offsets[None, None, :]) * bin_size[:, None, None]
        - 0.5
    )
    weights = jnp.maximum(
        0.0, 1.0 - jnp.abs(sample_points[..., None] - grid_points[None, None, None, :])
    )
    return jnp.mean(weights, axis=2)


def activate(values):
    return jax.nn.gelu(values, approximate=True)


def gelu_grad(values, incoming):
    return jax.vjp(activate, values)[1](incoming)[0]


def block_shape(proposal_count):
    block_size = 32
    return (block_size, proposal_count // block_size)


def crop_rows(own_map, row_weight, col_weight):
    height_cells, width_cells, channels = own_map.shape
    proposal_count = row_weight.shape[0]
    block_size, block_count = block_shape(proposal_count)
    flattened = jnp.transpose(own_map, (1, 0, 2)).reshape(width_cells, height_cells * channels)

    def per_block(blocks):
        row_part, col_part = blocks
        across = jnp.dot(
            col_part.reshape(block_size * POOL, width_cells),
            flattened,
            preferred_element_type=jnp.float32,
        )
        across = across.reshape(block_size, POOL, height_cells, channels)
        return jnp.einsum("riy,rjyc->rijc", row_part, across, precision=lax.Precision.HIGHEST)

    pooled = lax.map(
        per_block,
        (
            row_weight.reshape(block_count, block_size, POOL, height_cells),
            col_weight.reshape(block_count, block_size, POOL, width_cells),
        ),
    )
    return pooled.reshape(proposal_count, POOL * POOL * channels)


def crop_back(grad_pooled, row_weight, col_weight, channels):
    proposal_count, _, height_cells = row_weight.shape
    width_cells = col_weight.shape[2]
    block_size, block_count = block_shape(proposal_count)

    def per_block(running, blocks):
        row_part, col_part, grad_part = blocks
        grad_block = grad_part.reshape(block_size, POOL, POOL, channels)
        spread = jnp.einsum("riy,rijc->rjyc", row_part, grad_block, precision=lax.Precision.HIGHEST)
        added = lax.dot_general(
            col_part.astype(jnp.float32).reshape(block_size * POOL, width_cells),
            spread.reshape(block_size * POOL, height_cells * channels),
            (((0,), (0,)), ((), ())),
            precision=lax.Precision.HIGHEST,
            preferred_element_type=jnp.float32,
        )
        return (running + added, None)

    start = jnp.zeros((width_cells, height_cells * channels), jnp.float32)
    blocks = (
        row_weight.reshape(block_count, block_size, POOL, height_cells),
        col_weight.reshape(block_count, block_size, POOL, width_cells),
        grad_pooled.reshape(block_count, block_size, grad_pooled.shape[1]),
    )
    total, _ = lax.scan(per_block, start, blocks)
    return jnp.transpose(total.reshape(width_cells, height_cells, channels), (1, 0, 2))


def on_device(feature_map, proposals, hidden_weight, output_weight, upstream):
    own_map = feature_map[0]
    corners = proposals[0]
    own_height = own_map.shape[0]
    map_width = own_map.shape[1]
    channels = own_map.shape[2]
    row_offset = lax.axis_index("space") * own_height
    local_grid = (row_offset + jnp.arange(own_height, dtype=jnp.int32)).astype(jnp.float32)
    row_weight = axis_weights(corners[:, 0], corners[:, 2], local_grid)
    col_weight = axis_weights(
        corners[:, 1], corners[:, 3], jnp.arange(map_width, dtype=jnp.int32).astype(jnp.float32)
    ).astype(jnp.bfloat16)
    full_grid = jnp.arange(own_height * lax.axis_size("space"), dtype=jnp.int32).astype(jnp.float32)
    full_weight = axis_weights(corners[:, 0], corners[:, 2], full_grid)
    whole_map = lax.all_gather(own_map, "space", axis=0, tiled=True)
    pooled = crop_rows(whole_map, full_weight, col_weight).astype(jnp.bfloat16)
    pre_hidden = jnp.dot(pooled, hidden_weight, preferred_element_type=jnp.float32)
    hidden = activate(pre_hidden).astype(jnp.bfloat16)
    pre_output = lax.psum(
        jnp.dot(hidden, output_weight, preferred_element_type=jnp.float32).astype(jnp.bfloat16),
        "space",
    ).astype(jnp.float32)
    output_delta = gelu_grad(pre_output, upstream[0].astype(jnp.float32)).astype(jnp.bfloat16)
    step_second = lax.dot_general(
        hidden, output_delta, (((0,), (0,)), ((), ())), preferred_element_type=jnp.float32
    )
    second_total = lax.psum(step_second, "dp")
    hidden_back = lax.dot_general(
        output_delta, output_weight, (((1,), (1,)), ((), ())), preferred_element_type=jnp.float32
    )
    hidden_delta = gelu_grad(pre_hidden, hidden_back).astype(jnp.bfloat16)
    column_rows = lax.all_to_all(pooled, "dp", split_axis=1, concat_axis=0, tiled=True)
    delta_rows = lax.all_gather(hidden_delta, "dp", axis=0, tiled=True)
    first_total = lax.dot_general(
        column_rows, delta_rows, (((0,), (0,)), ((), ())), preferred_element_type=jnp.float32
    )
    partial_grad = lax.dot_general(
        hidden_delta, hidden_weight, (((1,), (1,)), ((), ())), preferred_element_type=jnp.float32
    )
    grad_share = lax.psum_scatter(
        partial_grad.astype(jnp.bfloat16), "space", scatter_dimension=0, tiled=True
    ).astype(jnp.float32)
    pooled_grad = lax.all_gather(
        grad_share.astype(jnp.bfloat16), "space", axis=0, tiled=True
    ).astype(grad_share.dtype)
    map_grad = crop_back(pooled_grad, row_weight, col_weight, channels)
    return (first_total, second_total, map_grad[None])


def solution(mesh):
    placed = (
        P("dp", "space", None, None),
        P("dp", None, None),
        P(None, "space"),
        P("space", None),
        P("dp", None, None),
    )
    return jax.shard_map(
        on_device,
        mesh=mesh,
        in_specs=placed,
        out_specs=(P("dp", "space"), P("space", None), P("dp", "space", None, None)),
        check_vma=False,
    )
```

profile of v0, /device:TPU:0, one launch (start us, length us, event | category | flops | bytes accessed | tf_op | source)
XLA Modules:
  0.0 361.1 jit_solution(6747203176717695255)
XLA Ops:
  7.2 0.8 convert_bitcast_fusion
  8.0 0.8 multiply_bitcast_fusion
  8.9 0.7 broadcast_add_fusion
  9.7 1.0 maximum_reduce_fusion
  11.3 16.2 %all-gather = bf16[1,24,84,256]{3,2,0,1:T(8,128)(2,1)S(1)} all-gather(bf16[1,12,84,256]{3,2,0,1:T(8,128)(2,1)} %bitcast.120), channel_id=2, replica_groups=mesh['dp'=16,'space'=2] {'space'}, dimensions={1}, use_global_device_ids=true | all-gather | bytes 1548288 | tf_op jit(solution)/shard_map/all_gather | solution.py:106
  28.0 34.6 %while.21 = (s32[]{:T(128)}, bf16[4,32,7,7,256]{4,2,3,1,0:T(8,128)(2,1)}, f32[4,32,7,24]{3,2,1,0:T(8,128)S(1)}, bf16[4,32,7,84]{3,1,0,2:T(8,128)(2,1)S(1)}, bf16[84,6144]{1,0:T(8,128)(2,1)S(1)}, /*index=5*/s32[]{:T(128)}) while((s32[]{:T(128)}, bf16[4,32,7,7,256]{4,2,3,1,0:T(8,128)(2,1)}, f32[4,32,7,24]{3,2,1,0:T(8,128)S(1)}, ...), condition=%wide.region_3.4_spmd, body=%wide.region_2.0_spmd.sunk | while | flops 346816512 | bytes 18293832 | solution.py:54
  28.3 0.9 fusion.66
  29.2 7.5 %bitcast_dynamic-update-slice_fusion.2 = bf16[4,32,7,7,256]{4,2,3,1,0:T(8,128)(2,1)} fusion(bf16[4,32,7,7,256]{4,2,3,1,0:T(8,128)(2,1)} %get-tuple-element.230, s32[]{:T(128)} %get-tuple-element.229, f32[32,7,24,256]{3,0,2,1:T(8,128)S(1)} %fusion.66, f32[4,32,7,24]{3,2,1,0:T(8,128)S(1)} %get-tuple-element.237), kind=kOutput, calls=%fused_computation.2.clone.1 | convolution fusion | flops 115605504 | bytes 7472128 | tf_op jit(solution)/shard_map/while/body/eval_jaxpr/riy,rjyc->rijc/dot_general | solution.py:52
  37.0 0.9 fusion.66
  37.8 7.5 %bitcast_dynamic-update-slice_fusion.2 = bf16[4,32,7,7,256]{4,2,3,1,0:T(8,128)(2,1)} fusion(bf16[4,32,7,7,256]{4,2,3,1,0:T(8,128)(2,1)} %get-tuple-element.230, s32[]{:T(128)} %get-tuple-element.229, f32[32,7,24,256]{3,0,2,1:T(8,128)S(1)} %fusion.66, f32[4,32,7,24]{3,2,1,0:T(8,128)S(1)} %get-tuple-element.237), kind=kOutput, calls=%fused_computation.2.clone.1 | convolution fusion | flops 115605504 | bytes 7472128 | tf_op jit(solution)/shard_map/while/body/eval_jaxpr/riy,rjyc->rijc/dot_general | solution.py:52
  45.7 0.9 fusion.66
  46.5 7.5 %bitcast_dynamic-update-slice_fusion.2 = bf16[4,32,7,7,256]{4,2,3,1,0:T(8,128)(2,1)} fusion(bf16[4,32,7,7,256]{4,2,3,1,0:T(8,128)(2,1)} %get-tuple-element.230, s32[]{:T(128)} %get-tuple-element.229, f32[32,7,24,256]{3,0,2,1:T(8,128)S(1)} %fusion.66, f32[4,32,7,24]{3,2,1,0:T(8,128)S(1)} %get-tuple-element.237), kind=kOutput, calls=%fused_computation.2.clone.1 | convolution fusion | flops 115605504 | bytes 7472128 | tf_op jit(solution)/shard_map/while/body/eval_jaxpr/riy,rjyc->rijc/dot_general | solution.py:52
  54.3 0.9 fusion.66
  55.2 7.5 %bitcast_dynamic-update-slice_fusion.2 = bf16[4,32,7,7,256]{4,2,3,1,0:T(8,128)(2,1)} fusion(bf16[4,32,7,7,256]{4,2,3,1,0:T(8,128)(2,1)} %get-tuple-element.230, s32[]{:T(128)} %get-tuple-element.229, f32[32,7,24,256]{3,0,2,1:T(8,128)S(1)} %fusion.66, f32[4,32,7,24]{3,2,1,0:T(8,128)S(1)} %get-tuple-element.237), kind=kOutput, calls=%fused_computation.2.clone.1 | convolution fusion | flops 115605504 | bytes 7472128 | tf_op jit(solution)/shard_map/while/body/eval_jaxpr/riy,rjyc->rijc/dot_general | solution.py:52
  62.6 5.1 %copy.77 = bf16[4,32,7,7,256]{4,3,2,1,0:T(8,128)(2,1)} copy(bf16[4,32,7,7,256]{4,2,3,1,0:T(8,128)(2,1)} %get-tuple-element.57) | data formatting | bytes 6422528 | tf_op jit(solution)/shard_map/convert_element_type | solution.py:107
  67.8 5.6 %convert_element_type.132 = bf16[128,12544]{1,0:T(8,128)(2,1)S(1)} reshape(bf16[4,32,7,7,256]{4,3,2,1,0:T(8,128)(2,1)} %copy.77) | data formatting | bytes 6422528 | tf_op jit(solution)/shard_map/convert_element_type | solution.py:107
  73.4 3.8 %fusion.39 = f32[128,256]{1,0:T(8,128)S(1)} fusion(bf16[128,12544]{1,0:T(8,128)(2,1)S(1)} %convert_element_type.132, bf16[12544,256]{1,0:T(8,128)(2,1)} %param.14), kind=kOutput, calls=%fused_computation.69 | convolution fusion | flops 822083584 | bytes 9764864 | tf_op jit(solution)/shard_map/dot_general | solution.py:108
  77.2 0.6 copy-done.4
  77.9 0.9 convolution_convert_fusion.1
  79.0 22.9 %all-reduce.3.cloned.1.call-done = bf16[128,512]{1,0:T(8,128)(2,1)} async-done(((bf16[128,512]{1,0:T(8,128)(2,1)}), bf16[128,512]{1,0:T(8,128)(2,1)}) %all-reduce.3.cloned.1.call-update) | async-done | bytes 131088 | tf_op jit(solution)/shard_map/psum | solution.py:110
  101.9 1.2 fusion.24
  103.1 0.6 copy-done.6
  103.7 1.1 fusion.37
  104.9 6.8 %convolution_convert_fusion = bf16[128,12544]{1,0:T(8,128)(2,1)} fusion(bf16[128,256]{1,0:T(8,128)(2,1)S(1)} %fusion.37, bf16[12544,256]{1,0:T(8,128)(2,1)} %param.14), kind=kOutput, calls=%fused_computation.21 | convolution fusion | flops 823689216 | bytes 9699328 | tf_op jit(solution)/shard_map/dot_general | solution.py:128
  111.7 9.3 %convert_element_type.129 = bf16[128,16,784]{2,1,0:T(8,128)(2,1)} reshape(bf16[4,32,7,7,256]{4,3,2,1,0:T(8,128)(2,1)} %copy.77) | data formatting | bytes 6422528 | tf_op jit(solution)/shard_map/convert_element_type | solution.py:107
  121.0 6.2 %copy.78 = bf16[128,16,784]{0,2,1:T(8,128)(2,1)} copy(bf16[128,16,784]{2,1,0:T(8,128)(2,1)} %convert_element_type.129) | data formatting | bytes 6422528 | tf_op jit(solution)/shard_map/convert_element_type | solution.py:107
  127.2 5.8 %all-to-all-start = ((bf16[128,16,784]{0,2,1:T(8,128)(2,1)}), bf16[128,16,784]{0,2,1:T(8,128)(2,1)S(1)}, u32[]{:S(2)}, u32[]{:S(2)}) async-start(bf16[128,16,784]{0,2,1:T(8,128)(2,1)} %copy.78), calls=%async_computation | async-start | bytes 6422528 | tf_op jit(solution)/shard_map/all_to_all | solution.py:123
  133.0 0.7 all-gather.4.cloned.1.call-update
  133.8 22.2 %reduce-scatter.2.cloned.1.call-done = bf16[64,12544]{1,0:T(8,128)(2,1)} async-done(((bf16[128,12544]{1,0:T(8,128)(2,1)}), bf16[64,12544]{1,0:T(8,128)(2,1)}) %reduce-scatter.2.cloned.1.call-update) | async-done | bytes 1605648 | tf_op jit(solution)/shard_map/reduce_scatter | solution.py:131
  156.1 0.9 copy.89
  157.2 1.0 copy.90
  158.2 2.0 fusion.38
  160.2 50.5 %all-gather.4.cloned.1.call-done = bf16[2048,256]{1,0:T(8,128)(2,1)} async-done(((bf16[128,256]{1,0:T(8,128)(2,1)}), bf16[2048,256]{1,0:T(8,128)(2,1)}) %all-gather.4.cloned.1.call-update) | async-done | bytes 1048592 | tf_op jit(solution)/shard_map/all_gather | solution.py:124
  210.8 3.1 fusion.18
  213.9 44.3 %all-gather.6.cloned.1.call-done = bf16[128,12544]{1,0:T(8,128)(2,1)} async-done(((bf16[64,12544]{1,0:T(8,128)(2,1)}), bf16[128,12544]{1,0:T(8,128)(2,1)}) %all-gather.6.cloned.1.call-update) | async-done | bytes 3211280 | tf_op jit(solution)/shard_map/all_gather | solution.py:134
  258.2 5.1 %convert.3 = f32[4,32,12544]{2,1,0:T(8,128)} convert(bf16[4,32,12544]{2,1,0:T(8,128)(2,1)} %bitcast.115) | non-fusion elementwise | flops 1605632 | bytes 9633792 | tf_op jit(solution)/shard_map/reshape | solution.py:86
  263.3 51.9 %while.22 = (s32[]{:T(128)}, f32[84,3072]{1,0:T(8,128)}, bf16[4,32,7,84]{3,2,1,0:T(8,128)(2,1)}, f32[4,32,12544]{2,1,0:T(8,128)}, f32[4,32,7,12]{3,2,1,0:T(8,128)}, /*index=5*/s32[]{:T(128)}, s32[]{:T(128)}) while((s32[]{:T(128)}, f32[84,3072]{1,0:T(8,128)}, bf16[4,32,7,84]{3,2,1,0:T(8,128)(2,1)}, f32[4,32,12544]{2,1,0:T(8,128)}, ...), condition=%wide.region_9.10_spmd.clone, body=%wide.region_8.9_spmd.clone.sunk | while | flops 751951872 | bytes 21422432 | solution.py:88
  263.3 1.5 constant_dynamic-slice_fusion.5
  264.8 0.4 reshape.239
  265.3 4.5 %fusion.71 = f32[32,7,256,12]{2,3,1,0:T(8,128)S(1)} fusion(f32[32,7,7,256]{3,2,1,0:T(8,128)S(1)} %reshape.239, f32[4,32,7,12]{3,2,1,0:T(8,128)} %get-tuple-element.259, s32[]{:T(128)} %get-tuple-element.248), kind=kOutput, calls=%fused_computation.14.clone.1 | convolution fusion | flops 57802752 | bytes 4489728 | tf_op jit(solution)/shard_map/while/body/eval_jaxpr/riy,rijc->rjyc/dot_general | solution.py:72
  269.8 2.4 copy.120
  272.2 0.9 constant_dynamic-slice_fusion.4
  273.1 2.2 convolution_add_fusion.2
  275.3 1.5 constant_dynamic-slice_fusion.5
  276.9 0.4 reshape.239
  277.3 4.5 %fusion.71 = f32[32,7,256,12]{2,3,1,0:T(8,128)S(1)} fusion(f32[32,7,7,256]{3,2,1,0:T(8,128)S(1)} %reshape.239, f32[4,32,7,12]{3,2,1,0:T(8,128)} %get-tuple-element.259, s32[]{:T(128)} %get-tuple-element.248), kind=kOutput, calls=%fused_computation.14.clone.1 | convolution fusion | flops 57802752 | bytes 4489728 | tf_op jit(solution)/shard_map/while/body/eval_jaxpr/riy,rijc->rjyc/dot_general | solution.py:72
  281.8 2.4 copy.120
  284.3 0.9 constant_dynamic-slice_fusion.4
  285.1 3.5 convolution_add_fusion.2
  288.6 1.5 constant_dynamic-slice_fusion.5
  290.1 0.4 reshape.239
  290.6 4.5 %fusion.71 = f32[32,7,256,12]{2,3,1,0:T(8,128)S(1)} fusion(f32[32,7,7,256]{3,2,1,0:T(8,128)S(1)} %reshape.239, f32[4,32,7,12]{3,2,1,0:T(8,128)} %get-tuple-element.259, s32[]{:T(128)} %get-tuple-element.248), kind=kOutput, calls=%fused_computation.14.clone.1 | convolution fusion | flops 57802752 | bytes 4489728 | tf_op jit(solution)/shard_map/while/body/eval_jaxpr/riy,rijc->rjyc/dot_general | solution.py:72
  295.1 2.4 copy.120
  297.5 0.9 constant_dynamic-slice_fusion.4
  298.4 3.5 convolution_add_fusion.2
  301.9 1.5 constant_dynamic-slice_fusion.5
  303.9 4.5 %fusion.71 = f32[32,7,256,12]{2,3,1,0:T(8,128)S(1)} fusion(f32[32,7,7,256]{3,2,1,0:T(8,128)S(1)} %reshape.239, f32[4,32,7,12]{3,2,1,0:T(8,128)} %get-tuple-element.259, s32[]{:T(128)} %get-tuple-element.248), kind=kOutput, calls=%fused_computation.14.clone.1 | convolution fusion | flops 57802752 | bytes 4489728 | tf_op jit(solution)/shard_map/while/body/eval_jaxpr/riy,rijc->rjyc/dot_general | solution.py:72
  308.4 2.4 copy.120
  310.8 0.9 constant_dynamic-slice_fusion.4
  311.7 3.5 convolution_add_fusion.2
  315.2 1.6 reshape.224
  316.8 2.0 copy.84
  318.8 33.9 %all-reduce.5.cloned.1.call-done = f32[256,512]{1,0:T(8,128)} async-done(((f32[256,512]{1,0:T(8,128)}), f32[256,512]{1,0:T(8,128)}) %all-reduce.5.cloned.1.call-update) | async-done | bytes 524304 | tf_op jit(solution)/shard_map/psum | solution.py:118
  352.7 1.9 copy.136
  (54 shorter events, 3.7 us)
Async XLA Ops:
  7.2 70.7 %copy-start = (bf16[256,512]{1,0:T(8,128)(2,1)S(1)}, bf16[256,512]{1,0:T(8,128)(2,1)}, u32[]{:S(2)}) copy-start(bf16[256,512]{1,0:T(8,128)(2,1)} %param.15) | copy-start | bytes 786436
  7.2 94.7 %all-reduce.3.cloned.1.call-start = ((), (), s32[]{:S(2)}) async-start(), calls=%async_computation.2 | async-start | bytes 262144 | tf_op jit(solution)/shard_map/psum | solution.py:110
  10.7 17.0 %copy-start.2 = (bf16[128,7,84]{0,2,1:T(8,128)(2,1)}, bf16[128,7,84]{0,2,1:T(8,128)(2,1)S(1)}, u32[]{:S(2)}) copy-start(bf16[128,7,84]{0,2,1:T(8,128)(2,1)S(1)} %multiply_convert_fusion) | copy-start | bytes 451588
  77.2 0.7 copy-start.4
  78.7 77.3 %reduce-scatter.2.cloned.1.call-start = ((), (), s32[]{:S(2)}) async-start(), calls=%async_computation.5 | async-start | bytes 4816896 | tf_op jit(solution)/shard_map/reduce_scatter | solution.py:131
  103.0 0.6 copy-start.6
  104.8 6.8 %copy-start.7 = (bf16[128,256]{1,0:T(8,128)(2,1)}, bf16[128,256]{1,0:T(8,128)(2,1)S(1)}, u32[]{:S(2)}) copy-start(bf16[128,256]{1,0:T(8,128)(2,1)S(1)} %fusion.37) | copy-start | bytes 196612
  127.2 28.8 %copy-start.3 = (bf16[128,7,84]{0,2,1:T(8,128)(2,1)S(1)}, bf16[128,7,84]{0,2,1:T(8,128)(2,1)}, u32[]{:S(2)}) copy-start(bf16[128,7,84]{0,2,1:T(8,128)(2,1)} %copy-done.2) | copy-start | bytes 451588
  127.2 31.0 %copy-start.5 = (f32[128,256]{1,0:T(8,128)S(1)}, f32[128,256]{1,0:T(8,128)}, u32[]{:S(2)}) copy-start(f32[128,256]{1,0:T(8,128)} %copy-done.4) | copy-start | bytes 393220
  127.2 83.6 %all-to-all-start = ((bf16[128,16,784]{0,2,1:T(8,128)(2,1)}), bf16[128,16,784]{0,2,1:T(8,128)(2,1)S(1)}, u32[]{:S(2)}, u32[]{:S(2)}) async-start(bf16[128,16,784]{0,2,1:T(8,128)(2,1)} %copy.78), calls=%async_computation | async-start | bytes 6422528 | tf_op jit(solution)/shard_map/all_to_all | solution.py:123
  133.0 77.8 %all-gather.4.cloned.1.call-start = ((), (), s32[]{:S(2)}) async-start(), calls=%async_computation.3 | async-start | bytes 1114112 | tf_op jit(solution)/shard_map/all_gather | solution.py:124
  133.7 124.4 %all-gather.6.cloned.1.call-start = ((), (), s32[]{:S(2)}) async-start(), calls=%async_computation.6 | async-start | bytes 4816896 | tf_op jit(solution)/shard_map/all_gather | solution.py:134
  156.0 196.7 %all-reduce.5.cloned.1.call-start = ((), (), s32[]{:S(2)}) async-start(), calls=%async_computation.4 | async-start | bytes 1048576 | tf_op jit(solution)/shard_map/psum | solution.py:118
  315.2 39.4 %copy-start.1 = (bf16[256,512]{1,0:T(8,128)(2,1)S(1)}, bf16[256,512]{1,0:T(8,128)(2,1)}, u32[]{:S(2)}) copy-start(bf16[256,512]{1,0:T(8,128)(2,1)} %param.15) | copy-start | bytes 786436
Sparse Core Ops, SparseCore 0:
  78.9 22.9 all-reduce.2
  111.8 44.1 reduce-scatter.1
  158.2 52.5 all-gather.3
  212.2 45.9 all-gather.5
  262.0 90.6 all-reduce.4
where the time goes:
time: 363 us; the launch traced here: 361 us
  waiting for transfers between devices  175 us (48%)
  matrix products  81.6 us (22%)
  local copies, waits for them, and re-layouts  58.4 us (16%)
  blocking collectives  16.2 us (4%)
  between operations  14 us (4%)
  other arithmetic  10.1 us (3%)
  starting transfers between devices  6.13 us (2%)
    all_gather x1, waiting for transfers between devices, on_device(): delta_rows = lax.all_gather(hidden_delta, 'dp', axis=0, tiled=True)  50.5 us
    all_gather x1, waiting for transfers between devices, on_device(): lax.all_gather(grad_share.astype(jnp.bfloat16), 'space', axis=0, tiled=True)  44.3 us
    psum x1, waiting for transfers between devices, on_device(): second_total = lax.psum(step_second, 'dp')  33.9 us
    dot_general x4, matrix products, per_block(): jnp.einsum('riy,rjyc->rijc', row_part, across, precision=lax.Precision.HI...  29.9 us
    convert_element_type x4, local copies, waits for them, and re-layouts, on_device(): pooled = crop_rows(whole_map, full_weight, col_weight).astype(jnp.bfloat16)  26.3 us
    psum x1, waiting for transfers between devices, on_device(): lax.psum(jnp.dot(hidden, output_weight, preferred_element_type=jnp.float3...  22.9 us
    reduce_scatter x1, waiting for transfers between devices, on_device(): lax.psum_scatter(partial_grad.astype(jnp.bfloat16), 'space', scatter_dime...  22.2 us
    dot_general x4, matrix products, per_block(): jnp.einsum('riy,rijc->rjyc', row_part, grad_block, precision=lax.Precisio...  17.9 us
  transfers between devices with their start and end apart: 6, of which 5 were waited for; matrix products, arithmetic and copies ran while one was open for 23% of the time, Pallas kernels for 0%

commit v1 on v0

--- a/solution.py
+++ b/solution.py
@@ -121,7 +121,14 @@
     )
     hidden_delta = gelu_grad(pre_hidden, hidden_back).astype(jnp.bfloat16)
     column_rows = lax.all_to_all(pooled, "dp", split_axis=1, concat_axis=0, tiled=True)
-    delta_rows = lax.all_gather(hidden_delta, "dp", axis=0, tiled=True)
+    size = lax.axis_size("dp")
+    route = [(i, (i + 1) % size) for i in range(size)]
+    pieces = [hidden_delta]
+    for far in range(1, size):
+        pieces = [lax.ppermute(pieces[0], "dp", route), *pieces]
+    out = jnp.concatenate(pieces, axis=0)
+    shift = (lax.axis_index("dp") + 1) * pieces[-1].shape[0]
+    delta_rows = jnp.roll(out, shift, axis=0)
     first_total = lax.dot_general(
         column_rows, delta_rows, (((0,), (0,)), ((), ())), preferred_element_type=jnp.float32
     )

time: 363 us -> 443 us (1.22)
  local copies, waits for them, and re-layouts: 58.4 us -> 99.9 us
  waiting for transfers between devices: 175 us -> 212 us
    ppermute x0 -> x15, waiting for transfers between devices: none -> 145 us  [on_device(): pieces = [lax.ppermute(pieces[0], 'dp', route), *pieces]]
    all_gather x1 -> x0, waiting for transfers between devices: 50.5 us -> none  [on_device(): delta_rows = lax.all_gather(hidden_delta, 'dp', axis=0, tiled=True)]
    all_gather x1, waiting for transfers between devices: 44.3 us -> 0.01 us  [on_device(): lax.all_gather(grad_share.astype(jnp.bfloat16), 'space', axis=0, tiled=True)]
    unnamed x21 -> x96, local copies, waits for them, and re-layouts: 6.54 us -> 47.3 us
    psum x1, waiting for transfers between devices: 33.9 us -> 0.01 us  [on_device(): second_total = lax.psum(step_second, 'dp')]
    reduce_scatter x1, waiting for transfers between devices: 22.2 us -> 44.2 us  [on_device(): lax.psum_scatter(partial_grad.astype(jnp.bfloat16), 'space', scatter_dime...]
  transfers between devices with their start and end apart: 6 -> 20, of which waited for: 5 -> 17; matrix products, arithmetic and copies ran while one was open for 23% -> 27% of each run, Pallas kernels for 0% -> 0%
where the time goes in v1:
time: 443 us; the launch traced here: 440 us
  waiting for transfers between devices  212 us (48%)
  local copies, waits for them, and re-layouts  99.9 us (23%)
  matrix products  81.6 us (18%)
  blocking collectives  15.9 us (4%)
  between operations  14.1 us (3%)
  other arithmetic  10.1 us (2%)
  starting transfers between devices  6.63 us (1%)
    ppermute x15, waiting for transfers between devices, on_device(): pieces = [lax.ppermute(pieces[0], 'dp', route), *pieces]  145 us
    unnamed x96, local copies, waits for them, and re-layouts  47.3 us
    reduce_scatter x1, waiting for transfers between devices, on_device(): lax.psum_scatter(partial_grad.astype(jnp.bfloat16), 'space', scatter_dime...  44.2 us
    dot_general x4, matrix products, per_block(): jnp.einsum('riy,rjyc->rijc', row_part, across, precision=lax.Precision.HI...  29.9 us
    convert_element_type x4, local copies, waits for them, and re-layouts, on_device(): pooled = crop_rows(whole_map, full_weight, col_weight).astype(jnp.bfloat16)  26.4 us
    psum x1, waiting for transfers between devices, on_device(): lax.psum(jnp.dot(hidden, output_weight, preferred_element_type=jnp.float3...  22.9 us
    dot_general x4, matrix products, per_block(): jnp.einsum('riy,rijc->rjyc', row_part, grad_block, precision=lax.Precisio...  17.9 us
    all_gather x1, blocking collectives, on_device(): whole_map = lax.all_gather(own_map, 'space', axis=0, tiled=True)  15.9 us
  transfers between devices with their start and end apart: 20, of which 17 were waited for; matrix products, arithmetic and copies ran while one was open for 27% of the time, Pallas kernels for 0%

profile of v1, /device:TPU:0, one launch (start us, length us, event | category | flops | bytes accessed | tf_op | source)
XLA Modules:
  0.0 440.4 jit_solution(5151289305594566156)
XLA Ops:
  11.3 15.9 %all-gather = bf16[1,24,84,256]{3,2,0,1:T(8,128)(2,1)S(1)} all-gather(bf16[1,12,84,256]{3,2,0,1:T(8,128)(2,1)S(1)} %bitcast.119), channel_id=2, replica_groups=mesh['dp'=16,'space'=2] {'space'}, dimensions={1}, use_global_device_ids=true | all-gather | bytes 1548288 | tf_op jit(solution)/shard_map/all_gather | solution.py:106
  27.8 34.6 %while.21 = (s32[]{:T(128)}, bf16[4,32,7,7,256]{4,2,3,1,0:T(8,128)(2,1)}, f32[4,32,7,24]{3,2,1,0:T(8,128)S(1)}, bf16[4,32,7,84]{3,1,0,2:T(8,128)(2,1)S(1)}, bf16[84,6144]{1,0:T(8,128)(2,1)S(1)}, /*index=5*/s32[]{:T(128)}) while((s32[]{:T(128)}, bf16[4,32,7,7,256]{4,2,3,1,0:T(8,128)(2,1)}, f32[4,32,7,24]{3,2,1,0:T(8,128)S(1)}, ...), condition=%wide.region_3.4_spmd, body=%wide.region_2.0_spmd.sunk | while | flops 346816512 | bytes 18293832 | solution.py:54
  29.0 7.5 %bitcast_dynamic-update-slice_fusion.2 = bf16[4,32,7,7,256]{4,2,3,1,0:T(8,128)(2,1)} fusion(bf16[4,32,7,7,256]{4,2,3,1,0:T(8,128)(2,1)} %get-tuple-element.230, s32[]{:T(128)} %get-tuple-element.229, f32[32,7,24,256]{3,0,2,1:T(8,128)S(1)} %fusion.67, f32[4,32,7,24]{3,2,1,0:T(8,128)S(1)} %get-tuple-element.237), kind=kOutput, calls=%fused_computation.2.clone.1 | convolution fusion | flops 115605504 | bytes 7472128 | tf_op jit(solution)/shard_map/while/body/eval_jaxpr/riy,rjyc->rijc/dot_general | solution.py:52
  37.6 7.5 %bitcast_dynamic-update-slice_fusion.2 = bf16[4,32,7,7,256]{4,2,3,1,0:T(8,128)(2,1)} fusion(bf16[4,32,7,7,256]{4,2,3,1,0:T(8,128)(2,1)} %get-tuple-element.230, s32[]{:T(128)} %get-tuple-element.229, f32[32,7,24,256]{3,0,2,1:T(8,128)S(1)} %fusion.67, f32[4,32,7,24]{3,2,1,0:T(8,128)S(1)} %get-tuple-element.237), kind=kOutput, calls=%fused_computation.2.clone.1 | convolution fusion | flops 115605504 | bytes 7472128 | tf_op jit(solution)/shard_map/while/body/eval_jaxpr/riy,rjyc->rijc/dot_general | solution.py:52
  46.3 7.5 %bitcast_dynamic-update-slice_fusion.2 = bf16[4,32,7,7,256]{4,2,3,1,0:T(8,128)(2,1)} fusion(bf16[4,32,7,7,256]{4,2,3,1,0:T(8,128)(2,1)} %get-tuple-element.230, s32[]{:T(128)} %get-tuple-element.229, f32[32,7,24,256]{3,0,2,1:T(8,128)S(1)} %fusion.67, f32[4,32,7,24]{3,2,1,0:T(8,128)S(1)} %get-tuple-element.237), kind=kOutput, calls=%fused_computation.2.clone.1 | convolution fusion | flops 115605504 | bytes 7472128 | tf_op jit(solution)/shard_map/while/body/eval_jaxpr/riy,rjyc->rijc/dot_general | solution.py:52
  54.9 7.5 %bitcast_dynamic-update-slice_fusion.2 = bf16[4,32,7,7,256]{4,2,3,1,0:T(8,128)(2,1)} fusion(bf16[4,32,7,7,256]{4,2,3,1,0:T(8,128)(2,1)} %get-tuple-element.230, s32[]{:T(128)} %get-tuple-element.229, f32[32,7,24,256]{3,0,2,1:T(8,128)S(1)} %fusion.67, f32[4,32,7,24]{3,2,1,0:T(8,128)S(1)} %get-tuple-element.237), kind=kOutput, calls=%fused_computation.2.clone.1 | convolution fusion | flops 115605504 | bytes 7472128 | tf_op jit(solution)/shard_map/while/body/eval_jaxpr/riy,rjyc->rijc/dot_general | solution.py:52
  62.4 5.1 %copy.77 = bf16[4,32,7,7,256]{4,3,2,1,0:T(8,128)(2,1)} copy(bf16[4,32,7,7,256]{4,2,3,1,0:T(8,128)(2,1)} %get-tuple-element.57) | data formatting | bytes 6422528 | tf_op jit(solution)/shard_map/convert_element_type | solution.py:107
  67.5 5.6 %convert_element_type.132 = bf16[128,12544]{1,0:T(8,128)(2,1)S(1)} reshape(bf16[4,32,7,7,256]{4,3,2,1,0:T(8,128)(2,1)} %copy.77) | data formatting | bytes 6422528 | tf_op jit(solution)/shard_map/convert_element_type | solution.py:107
  73.1 3.8 fusion.41
  78.7 22.9 %all-reduce.3.cloned.1.call-done = bf16[128,512]{1,0:T(8,128)(2,1)} async-done(((bf16[128,512]{1,0:T(8,128)(2,1)}), bf16[128,512]{1,0:T(8,128)(2,1)}) %all-reduce.3.cloned.1.call-update) | async-done | bytes 131088 | tf_op jit(solution)/shard_map/psum | solution.py:110
  105.3 6.8 %convolution_convert_fusion = bf16[128,12544]{1,0:T(8,128)(2,1)} fusion(bf16[128,256]{1,0:T(8,128)(2,1)S(1)} %fusion.38, bf16[12544,256]{1,0:T(8,128)(2,1)} %param.14), kind=kOutput, calls=%fused_computation.21 | convolution fusion | flops 823689216 | bytes 9699328 | tf_op jit(solution)/shard_map/dot_general | solution.py:135
  112.1 44.2 %reduce-scatter.2.cloned.1.call-done = bf16[64,12544]{1,0:T(8,128)(2,1)} async-done(((bf16[128,12544]{1,0:T(8,128)(2,1)}), bf16[64,12544]{1,0:T(8,128)(2,1)}) %reduce-scatter.2.cloned.1.call-update) | async-done | bytes 1605648 | tf_op jit(solution)/shard_map/reduce_scatter | solution.py:138
  156.4 9.3 %convert_element_type.129 = bf16[128,16,784]{2,1,0:T(8,128)(2,1)} reshape(bf16[4,32,7,7,256]{4,3,2,1,0:T(8,128)(2,1)} %copy.77) | data formatting | bytes 6422528 | tf_op jit(solution)/shard_map/convert_element_type | solution.py:107
  165.6 6.4 %copy.78 = bf16[128,16,784]{0,2,1:T(8,128)(2,1)} copy(bf16[128,16,784]{2,1,0:T(8,128)(2,1)} %convert_element_type.129) | data formatting | bytes 6422528 | tf_op jit(solution)/shard_map/convert_element_type | solution.py:107
  172.1 5.8 %all-to-all-start = ((bf16[128,16,784]{0,2,1:T(8,128)(2,1)}), bf16[128,16,784]{0,2,1:T(8,128)(2,1)S(1)}, u32[]{:S(2)}, u32[]{:S(2)}) async-start(bf16[128,16,784]{0,2,1:T(8,128)(2,1)} %copy.78), calls=%async_computation | async-start | bytes 6422528 | tf_op jit(solution)/shard_map/all_to_all | solution.py:123
  178.4 57.9 %collective-permute-done = bf16[128,256]{1,0:T(8,128)(2,1)S(1)} collective-permute-done((bf16[128,256]{1,0:T(8,128)(2,1)}, bf16[128,256]{1,0:T(8,128)(2,1)S(1)}, u32[]{:S(2)}, u32[]{:S(2)}) %collective-permute-start) | collective-permute-done | bytes 65568 | tf_op jit(solution)/shard_map/ppermute | solution.py:128
  237.0 6.5 %collective-permute-done.1 = bf16[128,256]{1,0:T(8,128)(2,1)S(1)} collective-permute-done((bf16[128,256]{1,0:T(8,128)(2,1)S(1)}, bf16[128,256]{1,0:T(8,128)(2,1)S(1)}, u32[]{:S(2)}, u32[]{:S(2)}) %collective-permute-start.1) | collective-permute-done | bytes 65568 | tf_op jit(solution)/shard_map/ppermute | solution.py:128
  244.1 6.5 %collective-permute-done.2 = bf16[128,256]{1,0:T(8,128)(2,1)S(1)} collective-permute-done((bf16[128,256]{1,0:T(8,128)(2,1)S(1)}, bf16[128,256]{1,0:T(8,128)(2,1)S(1)}, u32[]{:S(2)}, u32[]{:S(2)}) %collective-permute-start.2) | collective-permute-done | bytes 65568 | tf_op jit(solution)/shard_map/ppermute | solution.py:128
  251.2 6.4 %collective-permute-done.3 = bf16[128,256]{1,0:T(8,128)(2,1)S(1)} collective-permute-done((bf16[128,256]{1,0:T(8,128)(2,1)S(1)}, bf16[128,256]{1,0:T(8,128)(2,1)S(1)}, u32[]{:S(2)}, u32[]{:S(2)}) %collective-permute-start.3) | collective-permute-done | bytes 65568 | tf_op jit(solution)/shard_map/ppermute | solution.py:128
  258.2 6.4 %collective-permute-done.4 = bf16[128,256]{1,0:T(8,128)(2,1)S(1)} collective-permute-done((bf16[128,256]{1,0:T(8,128)(2,1)S(1)}, bf16[128,256]{1,0:T(8,128)(2,1)S(1)}, u32[]{:S(2)}, u32[]{:S(2)}) %collective-permute-start.4) | collective-permute-done | bytes 65568 | tf_op jit(solution)/shard_map/ppermute | solution.py:128
  265.2 6.4 %collective-permute-done.5 = bf16[128,256]{1,0:T(8,128)(2,1)S(1)} collective-permute-done((bf16[128,256]{1,0:T(8,128)(2,1)S(1)}, bf16[128,256]{1,0:T(8,128)(2,1)S(1)}, u32[]{:S(2)}, u32[]{:S(2)}) %collective-permute-start.5) | collective-permute-done | bytes 65568 | tf_op jit(solution)/shard_map/ppermute | solution.py:128
  272.2 6.4 %collective-permute-done.6 = bf16[128,256]{1,0:T(8,128)(2,1)S(1)} collective-permute-done((bf16[128,256]{1,0:T(8,128)(2,1)S(1)}, bf16[128,256]{1,0:T(8,128)(2,1)S(1)}, u32[]{:S(2)}, u32[]{:S(2)}) %collective-permute-start.6) | collective-permute-done | bytes 65568 | tf_op jit(solution)/shard_map/ppermute | solution.py:128
  279.3 6.4 %collective-permute-done.7 = bf16[128,256]{1,0:T(8,128)(2,1)S(1)} collective-permute-done((bf16[128,256]{1,0:T(8,128)(2,1)S(1)}, bf16[128,256]{1,0:T(8,128)(2,1)S(1)}, u32[]{:S(2)}, u32[]{:S(2)}) %collective-permute-start.7) | collective-permute-done | bytes 65568 | tf_op jit(solution)/shard_map/ppermute | solution.py:128
  286.3 6.4 %collective-permute-done.8 = bf16[128,256]{1,0:T(8,128)(2,1)S(1)} collective-permute-done((bf16[128,256]{1,0:T(8,128)(2,1)S(1)}, bf16[128,256]{1,0:T(8,128)(2,1)S(1)}, u32[]{:S(2)}, u32[]{:S(2)}) %collective-permute-start.8) | collective-permute-done | bytes 65568 | tf_op jit(solution)/shard_map/ppermute | solution.py:128
  293.3 6.5 %collective-permute-done.9 = bf16[128,256]{1,0:T(8,128)(2,1)} collective-permute-done((bf16[128,256]{1,0:T(8,128)(2,1)S(1)}, bf16[128,256]{1,0:T(8,128)(2,1)}, u32[]{:S(2)}, u32[]{:S(2)}) %collective-permute-start.9) | collective-permute-done | bytes 65568 | tf_op jit(solution)/shard_map/ppermute | solution.py:128
  299.8 6.7 %collective-permute-done.10 = bf16[128,256]{1,0:T(8,128)(2,1)} collective-permute-done((bf16[128,256]{1,0:T(8,128)(2,1)}, bf16[128,256]{1,0:T(8,128)(2,1)}, u32[]{:S(2)}, u32[]{:S(2)}) %collective-permute-start.10) | collective-permute-done | bytes 65568 | tf_op jit(solution)/shard_map/ppermute | solution.py:128
  306.5 6.6 %collective-permute-done.11 = bf16[128,256]{1,0:T(8,128)(2,1)S(1)} collective-permute-done((bf16[128,256]{1,0:T(8,128)(2,1)}, bf16[128,256]{1,0:T(8,128)(2,1)S(1)}, u32[]{:S(2)}, u32[]{:S(2)}) %collective-permute-start.11) | collective-permute-done | bytes 65568 | tf_op jit(solution)/shard_map/ppermute | solution.py:128
  313.9 6.3 %collective-permute-done.12 = bf16[128,256]{1,0:T(8,128)(2,1)} collective-permute-done((bf16[128,256]{1,0:T(8,128)(2,1)S(1)}, bf16[128,256]{1,0:T(8,128)(2,1)}, u32[]{:S(2)}, u32[]{:S(2)}) %collective-permute-start.12) | collective-permute-done | bytes 65568 | tf_op jit(solution)/shard_map/ppermute | solution.py:128
  322.2 4.7 %collective-permute-done.13 = bf16[128,256]{1,0:T(8,128)(2,1)} collective-permute-done((bf16[128,256]{1,0:T(8,128)(2,1)}, bf16[128,256]{1,0:T(8,128)(2,1)}, u32[]{:S(2)}, u32[]{:S(2)}) %collective-permute-start.13) | collective-permute-done | bytes 65568 | tf_op jit(solution)/shard_map/ppermute | solution.py:128
  326.9 2.0 fusion.40
  329.0 4.6 %collective-permute-done.14 = bf16[128,256]{1,0:T(8,128)(2,1)} collective-permute-done((bf16[128,256]{1,0:T(8,128)(2,1)}, bf16[128,256]{1,0:T(8,128)(2,1)}, u32[]{:S(2)}, u32[]{:S(2)}) %collective-permute-start.14) | collective-permute-done | bytes 65568 | tf_op jit(solution)/shard_map/ppermute | solution.py:128
  335.1 1.5 constant_dynamic-update-slice_fusion.30
  336.6 1.5 constant_dynamic-update-slice_fusion.29
  338.0 1.5 constant_dynamic-update-slice_fusion.28
  341.0 1.5 constant_dynamic-update-slice_fusion.26
  345.4 1.5 constant_dynamic-update-slice_fusion.23
  346.8 1.5 constant_dynamic-update-slice_fusion.22
  348.3 1.5 constant_dynamic-update-slice_fusion.21
  349.8 1.5 constant_dynamic-update-slice_fusion.20
  353.8 1.5 constant_dynamic-update-slice_fusion.15
  355.3 1.5 constant_dynamic-update-slice_fusion.14
  356.7 1.5 constant_dynamic-update-slice_fusion.13
  368.2 3.1 fusion.18
  371.3 5.1 %convert.3 = f32[4,32,12544]{2,1,0:T(8,128)} convert(bf16[4,32,12544]{2,1,0:T(8,128)(2,1)} %bitcast.114) | non-fusion elementwise | flops 1605632 | bytes 9633792 | tf_op jit(solution)/shard_map/reshape | solution.py:86
  376.4 51.9 %while.22 = (s32[]{:T(128)}, f32[84,3072]{1,0:T(8,128)}, bf16[4,32,7,84]{3,2,1,0:T(8,128)(2,1)}, f32[4,32,12544]{2,1,0:T(8,128)}, f32[4,32,7,12]{3,2,1,0:T(8,128)}, /*index=5*/s32[]{:T(128)}, s32[]{:T(128)}) while((s32[]{:T(128)}, f32[84,3072]{1,0:T(8,128)}, bf16[4,32,7,84]{3,2,1,0:T(8,128)(2,1)}, f32[4,32,12544]{2,1,0:T(8,128)}, ...), condition=%wide.region_9.10_spmd.clone, body=%wide.region_8.9_spmd.clone.sunk | while | flops 751951872 | bytes 21422432 | solution.py:88
  376.4 1.5 constant_dynamic-slice_fusion.5
  378.4 4.5 %fusion.72 = f32[32,7,256,12]{2,3,1,0:T(8,128)S(1)} fusion(f32[32,7,7,256]{3,2,1,0:T(8,128)S(1)} %reshape.239, f32[4,32,7,12]{3,2,1,0:T(8,128)} %get-tuple-element.259, s32[]{:T(128)} %get-tuple-element.248), kind=kOutput, calls=%fused_computation.14.clone.1 | convolution fusion | flops 57802752 | bytes 4489728 | tf_op jit(solution)/shard_map/while/body/eval_jaxpr/riy,rijc->rjyc/dot_general | solution.py:72
  382.9 2.4 copy.120
  386.2 2.2 convolution_add_fusion.2
  388.5 1.5 constant_dynamic-slice_fusion.5
  390.5 4.5 %fusion.72 = f32[32,7,256,12]{2,3,1,0:T(8,128)S(1)} fusion(f32[32,7,7,256]{3,2,1,0:T(8,128)S(1)} %reshape.239, f32[4,32,7,12]{3,2,1,0:T(8,128)} %get-tuple-element.259, s32[]{:T(128)} %get-tuple-element.248), kind=kOutput, calls=%fused_computation.14.clone.1 | convolution fusion | flops 57802752 | bytes 4489728 | tf_op jit(solution)/shard_map/while/body/eval_jaxpr/riy,rijc->rjyc/dot_general | solution.py:72
  394.9 2.4 copy.120
  398.3 3.5 convolution_add_fusion.2
  401.8 1.5 constant_dynamic-slice_fusion.5
  403.8 4.5 %fusion.72 = f32[32,7,256,12]{2,3,1,0:T(8,128)S(1)} fusion(f32[32,7,7,256]{3,2,1,0:T(8,128)S(1)} %reshape.239, f32[4,32,7,12]{3,2,1,0:T(8,128)} %get-tuple-element.259, s32[]{:T(128)} %get-tuple-element.248), kind=kOutput, calls=%fused_computation.14.clone.1 | convolution fusion | flops 57802752 | bytes 4489728 | tf_op jit(solution)/shard_map/while/body/eval_jaxpr/riy,rijc->rjyc/dot_general | solution.py:72
  408.2 2.4 copy.120
  411.6 3.5 convolution_add_fusion.2
  415.1 1.5 constant_dynamic-slice_fusion.5
  417.1 4.5 %fusion.72 = f32[32,7,256,12]{2,3,1,0:T(8,128)S(1)} fusion(f32[32,7,7,256]{3,2,1,0:T(8,128)S(1)} %reshape.239, f32[4,32,7,12]{3,2,1,0:T(8,128)} %get-tuple-element.259, s32[]{:T(128)} %get-tuple-element.248), kind=kOutput, calls=%fused_computation.14.clone.1 | convolution fusion | flops 57802752 | bytes 4489728 | tf_op jit(solution)/shard_map/while/body/eval_jaxpr/riy,rijc->rjyc/dot_general | solution.py:72
  421.5 2.4 copy.120
  424.9 3.5 convolution_add_fusion.2
  428.4 1.6 reshape.224
  430.0 2.0 copy.84
  432.0 1.9 copy.167
  (157 shorter events, 47.3 us)
Async XLA Ops:
  7.2 70.5 %copy-start = (bf16[256,512]{1,0:T(8,128)(2,1)S(1)}, bf16[256,512]{1,0:T(8,128)(2,1)}, u32[]{:S(2)}) copy-start(bf16[256,512]{1,0:T(8,128)(2,1)} %param.15) | copy-start | bytes 786436
  7.2 4.1 copy-start.8
  7.2 94.5 %all-reduce.3.cloned.1.call-start = ((), (), s32[]{:S(2)}) async-start(), calls=%async_computation.2 | async-start | bytes 262144 | tf_op jit(solution)/shard_map/psum | solution.py:110
  10.7 16.7 %copy-start.2 = (bf16[128,7,84]{0,2,1:T(8,128)(2,1)}, bf16[128,7,84]{0,2,1:T(8,128)(2,1)S(1)}, u32[]{:S(2)}) copy-start(bf16[128,7,84]{0,2,1:T(8,128)(2,1)S(1)} %multiply_convert_fusion) | copy-start | bytes 451588
  77.0 0.7 copy-start.4
  78.5 77.9 %reduce-scatter.2.cloned.1.call-start = ((), (), s32[]{:S(2)}) async-start(), calls=%async_computation.4 | async-start | bytes 4816896 | tf_op jit(solution)/shard_map/reduce_scatter | solution.py:138
  102.8 0.7 copy-start.9
  104.6 0.6 copy-start.6
  112.1 259.2 %all-gather.3.cloned.1.call-start = ((), (), s32[]{:S(2)}) async-start(), calls=%async_computation.5 | async-start | bytes 4816896 | tf_op jit(solution)/shard_map/all_gather | solution.py:141
  172.1 148.2 %copy-start.3 = (bf16[128,7,84]{0,2,1:T(8,128)(2,1)S(1)}, bf16[128,7,84]{0,2,1:T(8,128)(2,1)}, u32[]{:S(2)}) copy-start(bf16[128,7,84]{0,2,1:T(8,128)(2,1)} %copy-done.2) | copy-start | bytes 451588
  172.1 154.8 %copy-start.5 = (f32[128,256]{1,0:T(8,128)S(1)}, f32[128,256]{1,0:T(8,128)}, u32[]{:S(2)}) copy-start(f32[128,256]{1,0:T(8,128)} %copy-done.4) | copy-start | bytes 393220
  172.1 196.1 %all-to-all-start = ((bf16[128,16,784]{0,2,1:T(8,128)(2,1)}), bf16[128,16,784]{0,2,1:T(8,128)(2,1)S(1)}, u32[]{:S(2)}, u32[]{:S(2)}) async-start(bf16[128,16,784]{0,2,1:T(8,128)(2,1)} %copy.78), calls=%async_computation | async-start | bytes 6422528 | tf_op jit(solution)/shard_map/all_to_all | solution.py:123
  177.9 254.1 %all-reduce.5.cloned.1.call-start = ((), (), s32[]{:S(2)}) async-start(), calls=%async_computation.3 | async-start | bytes 1048576 | tf_op jit(solution)/shard_map/psum | solution.py:118
  177.9 58.4 %collective-permute-start = (bf16[128,256]{1,0:T(8,128)(2,1)}, bf16[128,256]{1,0:T(8,128)(2,1)S(1)}, u32[]{:S(2)}, u32[]{:S(2)}) collective-permute-start(bf16[128,256]{1,0:T(8,128)(2,1)} %copy-done.6), channel_id=1, source_target_pairs={{0,2},{2,4},{4,6},{6,8},{8,10},{10,12},{12,14},{14,16},{16,18},{18... | collective-permute-start | bytes 196616 | tf_op jit(solution)/shard_map/ppermute | solution.py:128
  236.3 0.6 copy-start.10
  237.0 6.5 %collective-permute-start.1 = (bf16[128,256]{1,0:T(8,128)(2,1)S(1)}, bf16[128,256]{1,0:T(8,128)(2,1)S(1)}, u32[]{:S(2)}, u32[]{:S(2)}) collective-permute-start(bf16[128,256]{1,0:T(8,128)(2,1)S(1)} %collective-permute-done), channel_id=1, source_target_pairs={{0,2},{2,4},{4,6},{6,8},{8,10},{10,12},{12,14},{14,16},{16,18},{18... | collective-permute-start | bytes 196616 | tf_op jit(solution)/shard_map/ppermute | solution.py:128
  243.4 0.6 copy-start.12
  244.1 6.5 %collective-permute-start.2 = (bf16[128,256]{1,0:T(8,128)(2,1)S(1)}, bf16[128,256]{1,0:T(8,128)(2,1)S(1)}, u32[]{:S(2)}, u32[]{:S(2)}) collective-permute-start(bf16[128,256]{1,0:T(8,128)(2,1)S(1)} %collective-permute-done.1), channel_id=1, source_target_pairs={{0,2},{2,4},{4,6},{6,8},{8,10},{10,12},{12,14},{14,16},{16,18},{18... | collective-permute-start | bytes 196616 | tf_op jit(solution)/shard_map/ppermute | solution.py:128
  250.6 0.6 copy-start.14
  251.2 6.4 %collective-permute-start.3 = (bf16[128,256]{1,0:T(8,128)(2,1)S(1)}, bf16[128,256]{1,0:T(8,128)(2,1)S(1)}, u32[]{:S(2)}, u32[]{:S(2)}) collective-permute-start(bf16[128,256]{1,0:T(8,128)(2,1)S(1)} %collective-permute-done.2), channel_id=1, source_target_pairs={{0,2},{2,4},{4,6},{6,8},{8,10},{10,12},{12,14},{14,16},{16,18},{18... | collective-permute-start | bytes 196616 | tf_op jit(solution)/shard_map/ppermute | solution.py:128
  257.6 0.6 copy-start.16
  258.2 6.4 %collective-permute-start.4 = (bf16[128,256]{1,0:T(8,128)(2,1)S(1)}, bf16[128,256]{1,0:T(8,128)(2,1)S(1)}, u32[]{:S(2)}, u32[]{:S(2)}) collective-permute-start(bf16[128,256]{1,0:T(8,128)(2,1)S(1)} %collective-permute-done.3), channel_id=1, source_target_pairs={{0,2},{2,4},{4,6},{6,8},{8,10},{10,12},{12,14},{14,16},{16,18},{18... | collective-permute-start | bytes 196616 | tf_op jit(solution)/shard_map/ppermute | solution.py:128
  264.6 0.6 copy-start.18
  265.2 6.4 %collective-permute-start.5 = (bf16[128,256]{1,0:T(8,128)(2,1)S(1)}, bf16[128,256]{1,0:T(8,128)(2,1)S(1)}, u32[]{:S(2)}, u32[]{:S(2)}) collective-permute-start(bf16[128,256]{1,0:T(8,128)(2,1)S(1)} %collective-permute-done.4), channel_id=1, source_target_pairs={{0,2},{2,4},{4,6},{6,8},{8,10},{10,12},{12,14},{14,16},{16,18},{18... | collective-permute-start | bytes 196616 | tf_op jit(solution)/shard_map/ppermute | solution.py:128
  271.6 0.6 copy-start.20
  272.2 6.4 %collective-permute-start.6 = (bf16[128,256]{1,0:T(8,128)(2,1)S(1)}, bf16[128,256]{1,0:T(8,128)(2,1)S(1)}, u32[]{:S(2)}, u32[]{:S(2)}) collective-permute-start(bf16[128,256]{1,0:T(8,128)(2,1)S(1)} %collective-permute-done.5), channel_id=1, source_target_pairs={{0,2},{2,4},{4,6},{6,8},{8,10},{10,12},{12,14},{14,16},{16,18},{18... | collective-permute-start | bytes 196616 | tf_op jit(solution)/shard_map/ppermute | solution.py:128
  278.6 0.6 copy-start.22
  279.2 6.4 %collective-permute-start.7 = (bf16[128,256]{1,0:T(8,128)(2,1)S(1)}, bf16[128,256]{1,0:T(8,128)(2,1)S(1)}, u32[]{:S(2)}, u32[]{:S(2)}) collective-permute-start(bf16[128,256]{1,0:T(8,128)(2,1)S(1)} %collective-permute-done.6), channel_id=1, source_target_pairs={{0,2},{2,4},{4,6},{6,8},{8,10},{10,12},{12,14},{14,16},{16,18},{18... | collective-permute-start | bytes 196616 | tf_op jit(solution)/shard_map/ppermute | solution.py:128
  285.6 0.6 copy-start.24
  286.3 6.4 %collective-permute-start.8 = (bf16[128,256]{1,0:T(8,128)(2,1)S(1)}, bf16[128,256]{1,0:T(8,128)(2,1)S(1)}, u32[]{:S(2)}, u32[]{:S(2)}) collective-permute-start(bf16[128,256]{1,0:T(8,128)(2,1)S(1)} %collective-permute-done.7), channel_id=1, source_target_pairs={{0,2},{2,4},{4,6},{6,8},{8,10},{10,12},{12,14},{14,16},{16,18},{18... | collective-permute-start | bytes 196616 | tf_op jit(solution)/shard_map/ppermute | solution.py:128
  292.7 0.6 copy-start.26
  293.3 6.5 %collective-permute-start.9 = (bf16[128,256]{1,0:T(8,128)(2,1)S(1)}, bf16[128,256]{1,0:T(8,128)(2,1)}, u32[]{:S(2)}, u32[]{:S(2)}) collective-permute-start(bf16[128,256]{1,0:T(8,128)(2,1)S(1)} %collective-permute-done.8), channel_id=1, source_target_pairs={{0,2},{2,4},{4,6},{6,8},{8,10},{10,12},{12,14},{14,16},{16,18},{18... | collective-permute-start | bytes 196616 | tf_op jit(solution)/shard_map/ppermute | solution.py:128
  299.8 6.7 %collective-permute-start.10 = (bf16[128,256]{1,0:T(8,128)(2,1)}, bf16[128,256]{1,0:T(8,128)(2,1)}, u32[]{:S(2)}, u32[]{:S(2)}) collective-permute-start(bf16[128,256]{1,0:T(8,128)(2,1)} %collective-permute-done.9), channel_id=1, source_target_pairs={{0,2},{2,4},{4,6},{6,8},{8,10},{10,12},{12,14},{14,16},{16,18},{18... | collective-permute-start | bytes 196616 | tf_op jit(solution)/shard_map/ppermute | solution.py:128
  306.5 6.6 %collective-permute-start.11 = (bf16[128,256]{1,0:T(8,128)(2,1)}, bf16[128,256]{1,0:T(8,128)(2,1)S(1)}, u32[]{:S(2)}, u32[]{:S(2)}) collective-permute-start(bf16[128,256]{1,0:T(8,128)(2,1)} %collective-permute-done.10), channel_id=1, source_target_pairs={{0,2},{2,4},{4,6},{6,8},{8,10},{10,12},{12,14},{14,16},{16,18},{18... | collective-permute-start | bytes 196616 | tf_op jit(solution)/shard_map/ppermute | solution.py:128
  313.1 0.6 copy-start.28
  313.7 6.5 %collective-permute-start.12 = (bf16[128,256]{1,0:T(8,128)(2,1)S(1)}, bf16[128,256]{1,0:T(8,128)(2,1)}, u32[]{:S(2)}, u32[]{:S(2)}) collective-permute-start(bf16[128,256]{1,0:T(8,128)(2,1)S(1)} %collective-permute-done.11), channel_id=1, source_target_pairs={{0,2},{2,4},{4,6},{6,8},{8,10},{10,12},{12,14},{14,16},{16,18},{18... | collective-permute-start | bytes 196616 | tf_op jit(solution)/shard_map/ppermute | solution.py:128
  320.2 6.7 %collective-permute-start.13 = (bf16[128,256]{1,0:T(8,128)(2,1)}, bf16[128,256]{1,0:T(8,128)(2,1)}, u32[]{:S(2)}, u32[]{:S(2)}) collective-permute-start(bf16[128,256]{1,0:T(8,128)(2,1)} %collective-permute-done.12), channel_id=1, source_target_pairs={{0,2},{2,4},{4,6},{6,8},{8,10},{10,12},{12,14},{14,16},{16,18},{18... | collective-permute-start | bytes 196616 | tf_op jit(solution)/shard_map/ppermute | solution.py:128
  321.1 31.4 %copy-start.11 = (bf16[128,256]{1,0:T(8,128)(2,1)S(1)}, bf16[128,256]{1,0:T(8,128)(2,1)}, u32[]{:S(2)}) copy-start(bf16[128,256]{1,0:T(8,128)(2,1)} %copy-done.10) | copy-start | bytes 196612
  321.1 32.0 %copy-start.7 = (bf16[128,256]{1,0:T(8,128)(2,1)S(1)}, bf16[128,256]{1,0:T(8,128)(2,1)}, u32[]{:S(2)}) copy-start(bf16[128,256]{1,0:T(8,128)(2,1)} %copy-done.6) | copy-start | bytes 196612
  326.9 6.7 %collective-permute-start.14 = (bf16[128,256]{1,0:T(8,128)(2,1)}, bf16[128,256]{1,0:T(8,128)(2,1)}, u32[]{:S(2)}, u32[]{:S(2)}) collective-permute-start(bf16[128,256]{1,0:T(8,128)(2,1)} %collective-permute-done.13), channel_id=1, source_target_pairs={{0,2},{2,4},{4,6},{6,8},{8,10},{10,12},{12,14},{14,16},{16,18},{18... | collective-permute-start | bytes 196616 | tf_op jit(solution)/shard_map/ppermute | solution.py:128
  328.9 22.4 %copy-start.15 = (bf16[128,256]{1,0:T(8,128)(2,1)S(1)}, bf16[128,256]{1,0:T(8,128)(2,1)}, u32[]{:S(2)}) copy-start(bf16[128,256]{1,0:T(8,128)(2,1)} %copy-done.14) | copy-start | bytes 196612
  328.9 23.0 %copy-start.13 = (bf16[128,256]{1,0:T(8,128)(2,1)S(1)}, bf16[128,256]{1,0:T(8,128)(2,1)}, u32[]{:S(2)}) copy-start(bf16[128,256]{1,0:T(8,128)(2,1)} %copy-done.12) | copy-start | bytes 196612
  328.9 36.1 %copy-start.17 = (bf16[128,256]{1,0:T(8,128)(2,1)S(1)}, bf16[128,256]{1,0:T(8,128)(2,1)}, u32[]{:S(2)}) copy-start(bf16[128,256]{1,0:T(8,128)(2,1)} %copy-done.16) | copy-start | bytes 196612
  328.9 29.3 %copy-start.29 = (bf16[128,256]{1,0:T(8,128)(2,1)S(1)}, bf16[128,256]{1,0:T(8,128)(2,1)}, u32[]{:S(2)}) copy-start(bf16[128,256]{1,0:T(8,128)(2,1)} %copy-done.28) | copy-start | bytes 196612
  328.9 32.9 %copy-start.27 = (bf16[128,256]{1,0:T(8,128)(2,1)S(1)}, bf16[128,256]{1,0:T(8,128)(2,1)}, u32[]{:S(2)}) copy-start(bf16[128,256]{1,0:T(8,128)(2,1)} %copy-done.26) | copy-start | bytes 196612
  328.9 33.5 %copy-start.25 = (bf16[128,256]{1,0:T(8,128)(2,1)S(1)}, bf16[128,256]{1,0:T(8,128)(2,1)}, u32[]{:S(2)}) copy-start(bf16[128,256]{1,0:T(8,128)(2,1)} %copy-done.24) | copy-start | bytes 196612
  328.9 34.1 %copy-start.23 = (bf16[128,256]{1,0:T(8,128)(2,1)S(1)}, bf16[128,256]{1,0:T(8,128)(2,1)}, u32[]{:S(2)}) copy-start(bf16[128,256]{1,0:T(8,128)(2,1)} %copy-done.22) | copy-start | bytes 196612
  329.0 34.7 %copy-start.21 = (bf16[128,256]{1,0:T(8,128)(2,1)S(1)}, bf16[128,256]{1,0:T(8,128)(2,1)}, u32[]{:S(2)}) copy-start(bf16[128,256]{1,0:T(8,128)(2,1)} %copy-done.20) | copy-start | bytes 196612
  329.0 35.4 %copy-start.19 = (bf16[128,256]{1,0:T(8,128)(2,1)S(1)}, bf16[128,256]{1,0:T(8,128)(2,1)}, u32[]{:S(2)}) copy-start(bf16[128,256]{1,0:T(8,128)(2,1)} %copy-done.18) | copy-start | bytes 196612
  428.4 5.5 %copy-start.1 = (bf16[256,512]{1,0:T(8,128)(2,1)S(1)}, bf16[256,512]{1,0:T(8,128)(2,1)}, u32[]{:S(2)}) copy-start(bf16[256,512]{1,0:T(8,128)(2,1)} %param.15) | copy-start | bytes 786436
Sparse Core Ops, SparseCore 0:
  78.6 23.0 all-reduce.2
  112.2 44.1 reduce-scatter.1
  157.9 45.6 all-gather.2
  329.0 90.9 all-reduce.4
